TPU v7x, 32 devices: a whole 2x2x4 slice. The times are simulated.
32 devices in a mesh: tm: 8 (over z, y), coef: 4 (over x, core).
Axes of the slice: x: 2, y: 2, z: 4, core: 2. Of those that a mesh axis runs over, the one named last changes fastest.
Arguments:
- design: bfloat16 [2048, 50176], P('tm', 'coef'), may hold values from -0.0390625 to 0.0390625
- observed: float32 [2048, 128], P('tm'), may hold values from -6 to 6
- slab_counts: int32 [8], P('tm'), may hold values from 128 to 256, as said below
- gap_mask: int32 [2048], P('tm'), may hold values 0 or 1
- filter_taps: float32 [128], replicated, may hold values from -0.5 to 1.2, as said below
- kaula_diag: float32 [50176], P('coef'), may hold values from 0.1 to 1
- precond: float32 [50176], P('coef'), may hold values from 0.3 to 3
Outputs:
- solution: float32 [50176, 128], P(('coef', 'tm'))
- residual: float32 [50176, 128], P(('coef', 'tm'))
Inputs may be any that keep to these rules, and one draw needn't show every extreme that they name: `slab_counts`: every slab holds at most 256 valid epochs, and some slab holds exactly 256. filter_taps[0] lies between 1 and 1.2.
All inputs are finite; a program needn't handle non-finite values. No bound on the sum of `gap_mask` on one device may be relied on, other than what follows from the above.
Results may differ from a plain program's by a relative error of at most 0.0065.
The roundings to bfloat16 on the way count: a program that leaves them out, or rounds other values in their place, can miss the bound.
Values may be sent and summed in bfloat16 or wider, within the bound.
No kernel may reach another device: no remote copies, remote signals or barrier semaphores. Data moves between devices by JAX's collectives and lax.ppermute only.
A program may use at most 64 MiB of HBM per device.

v0:
```python
import jax
import jax.numpy as jnp
from jax import lax
from jax.sharding import PartitionSpec as P

ITERS = 2


def shifted(value, axis, steps):
    count = lax.axis_size(axis)
    first, last = (max(0, -steps), min(count, count - steps))
    return lax.ppermute(value, axis, [(source, source + steps) for source in range(first, last)])


def toeplitz(pattern, band_len):
    tiled = jnp.tile(pattern, band_len)[: band_len * (2 * band_len - 1)]
    return tiled.reshape(band_len, 2 * band_len - 1)[:, :band_len]


def block_pair(filter_taps):
    band_len = filter_taps.shape[0]
    spacer = jnp.zeros((band_len,), jnp.float32)
    reversed_taps = filter_taps[:0:-1]
    lower = jnp.concatenate([filter_taps[:1], spacer, reversed_taps])
    upper = jnp.concatenate([jnp.zeros((1,), jnp.float32), reversed_taps, spacer])
    return (toeplitz(lower, band_len), toeplitz(upper, band_len))


def forward(values, lower_block, upper_block):
    band_len = lower_block.shape[0]
    blocks = values.reshape(-1, band_len, values.shape[1])
    tail_block = shifted(blocks[-1], "tm", 1)
    previous = jnp.concatenate([tail_block[None], blocks[:-1]], 0)
    result = jnp.einsum("ij,bjr->bir", lower_block, blocks, precision=lax.Precision.HIGHEST)
    result = result + jnp.einsum(
        "ij,bjr->bir", upper_block, previous, precision=lax.Precision.HIGHEST
    )
    return result.reshape(values.shape)


def backward(values, lower_block, upper_block):
    band_len = lower_block.shape[0]
    blocks = values.reshape(-1, band_len, values.shape[1])
    head_block = shifted(blocks[0], "tm", -1)
    following = jnp.concatenate([blocks[1:], head_block[None]], 0)
    result = jnp.einsum("ji,bjr->bir", lower_block, blocks, precision=lax.Precision.HIGHEST)
    result = result + jnp.einsum(
        "ji,bjr->bir", upper_block, following, precision=lax.Precision.HIGHEST
    )
    return result.reshape(values.shape)


def shards(design, observed, slab_counts, gap_mask, filter_taps, kaula_diag, precond):
    epoch_rows, coef_rows = design.shape
    owned_rows = coef_rows // lax.axis_size("tm")
    owner_index = lax.axis_index("tm")
    lower_block, upper_block = block_pair(filter_taps)
    position = jnp.arange(epoch_rows, dtype=jnp.int32)
    weight = ((gap_mask == 1) & (position < slab_counts[0])).astype(jnp.float32)[:, None]

    def weighted(values):
        inner = forward(weight * values, lower_block, upper_block)
        return (weight * backward(inner, lower_block, upper_block)).astype(jnp.bfloat16)

    def transposed_term(filtered):
        return lax.dot_general(
            design, filtered, (((0,), (0,)), ((), ())), preferred_element_type=jnp.float32
        )

    def collect_rows(filtered):
        return lax.psum_scatter(transposed_term(filtered), "tm", scatter_dimension=0, tiled=True)

    def global_sum(terms):
        return lax.psum(terms, ("tm", "coef"))

    kaula_col = lax.dynamic_slice_in_dim(kaula_diag, owner_index * owned_rows, owned_rows, 0)[
        :, None
    ]
    precond_col = lax.dynamic_slice_in_dim(precond, owner_index * owned_rows, owned_rows, 0)[
        :, None
    ]
    residual = collect_rows(weighted(observed))
    solution = jnp.zeros_like(residual)
    scaled = precond_col * residual
    direction = scaled
    norm_now = global_sum(jnp.sum(residual * scaled, 0))
    for iteration in range(ITERS):
        slab_values = lax.psum(
            jnp.dot(
                design,
                lax.all_gather(direction.astype(jnp.bfloat16), "tm", axis=0, tiled=True),
                preferred_element_type=jnp.float32,
            ),
            "coef",
        )
        image = collect_rows(weighted(slab_values)) + kaula_col * direction
        curvature = global_sum(jnp.sum(direction * image, 0))
        step_len = norm_now / curvature
        solution = solution + step_len * direction
        residual = residual - step_len * image
        if iteration + 1 < ITERS:
            scaled = precond_col * residual
            norm_next = global_sum(jnp.sum(residual * scaled, 0))
            direction = scaled + norm_next / norm_now * direction
            norm_now = norm_next
    return (solution, residual)


def solution(mesh):
    placed = (P("tm", "coef"), P("tm", None), P("tm"), P("tm"), P(), P("coef"), P("coef"))
    return jax.shard_map(
        shards,
        mesh=mesh,
        in_specs=placed,
        out_specs=(P(("coef", "tm"), None), P(("coef", "tm"), None)),
        check_vma=False,
    )
```

profile of v0, /device:TPU:0, one launch (start us, length us, event | category | flops | bytes accessed | tf_op | source)
XLA Modules:
  0.0 791.0 jit_solution(16113411345253262551)
XLA Ops:
  7.9 1.0 copy.30
  8.9 0.7 and_convert_fusion
  9.6 4.9 collective-permute-start
  14.5 0.7 slice.67
  15.3 0.7 pad_maximum_fusion.1
  16.1 0.3 reshape.46
  16.5 0.3 fusion.14
  16.8 0.3 reshape.47
  17.2 0.3 fusion.2
  17.5 1.3 collective-permute-start.1
  18.8 0.3 fusion.40
  19.1 4.5 collective-permute-done.1
  23.7 0.3 convolution_add_fusion.4
  24.1 6.5 convolution_bitcast_fusion.2
  30.6 8.0 %copy.74 = f32[12544,128]{1,0:T(8,128)} copy(f32[12544,128]{0,1:T(8,128)} %convolution_bitcast_fusion.2) | data formatting | bytes 12845056
  38.7 0.8 dynamic_slice.6
  39.4 120.5 %reduce-scatter.10.cloned.1.call-done = f32[1568,128]{1,0:T(8,128)} async-done(((f32[12544,128]{1,0:T(8,128)}), f32[1568,128]{1,0:T(8,128)}) %reduce-scatter.10.cloned.1.call-update) | async-done | bytes 802832
  159.9 1.4 copy.75
  161.4 0.9 copy.37
  162.4 60.2 %all-gather.3.cloned.1.call-done = bf16[12544,128]{1,0:T(8,128)(2,1)} async-done(((bf16[1568,128]{1,0:T(8,128)(2,1)}), bf16[12544,128]{1,0:T(8,128)(2,1)}) %all-gather.3.cloned.1.call-update) | async-done | bytes 3211280 | tf_op jit(solution)/shard_map/all_gather | solution.py:91
  222.6 6.7 convolution_bitcast_fusion.4
  229.3 30.5 %all-reduce.4.cloned.1.call-done = f32[256,128]{0,1:T(8,128)} async-done(((f32[256,128]{0,1:T(8,128)}), f32[256,128]{0,1:T(8,128)}) %all-reduce.4.cloned.1.call-update) | async-done | bytes 131088 | tf_op jit(solution)/shard_map/psum | solution.py:88
  259.9 0.9 broadcast_multiply_fusion.1
  260.8 3.4 collective-permute-start.2
  264.2 1.2 fusion.11
  265.4 0.7 collective-permute-done.2
  266.1 0.3 fusion.1
  266.4 1.3 collective-permute-start.3
  267.7 0.3 fusion.39
  268.0 4.9 collective-permute-done.3
  272.9 0.3 convolution_add_fusion.2
  273.3 6.5 convolution_bitcast_fusion.1
  279.8 8.0 %copy.76 = f32[12544,128]{1,0:T(8,128)} copy(f32[12544,128]{0,1:T(8,128)} %convolution_bitcast_fusion.1) | data formatting | bytes 12845056
  287.9 0.8 dynamic_slice.7
  288.7 119.7 %reduce-scatter.12.cloned.1.call-done = f32[1568,128]{1,0:T(8,128)} async-done(((f32[12544,128]{1,0:T(8,128)}), f32[1568,128]{1,0:T(8,128)}) %reduce-scatter.12.cloned.1.call-update) | async-done | bytes 802832
  408.4 1.4 copy.77
  409.9 0.3 fusion.5
  410.2 39.5 %all-reduce = (f32[128]{0:T(128)S(1)}, f32[128]{0:T(128)S(1)}) all-reduce(f32[128]{0:T(128)S(1)} %get-tuple-element.7, f32[128]{0:T(128)S(1)} %get-tuple-element.6), channel_id=1, replica_groups=mesh['tm'=8,'coef'=4] {'tm','coef'}, use_global_device_ids=true, to_apply=%region_2.0 | all-reduce | flops 256 | bytes 2048 | tf_op jit(solution)/shard_map/psum | solution.py:74
  449.7 0.3 fusion.7
  450.0 39.6 %psum.45 = f32[128]{0:T(128)S(1)} all-reduce(f32[128]{0:T(128)S(1)} %fusion.7), channel_id=1, replica_groups=mesh['tm'=8,'coef'=4] {'tm','coef'}, use_global_device_ids=true, to_apply=%region_8.0 | all-reduce | flops 128 | bytes 1024 | tf_op jit(solution)/shard_map/psum | solution.py:74
  489.6 0.3 fusion.47
  490.0 0.9 copy.44
  490.9 0.2 all-reduce.6.cloned.1.call-start
  491.2 60.7 %all-gather.5.cloned.1.call-done = bf16[12544,128]{1,0:T(8,128)(2,1)} async-done(((bf16[1568,128]{1,0:T(8,128)(2,1)}), bf16[12544,128]{1,0:T(8,128)(2,1)}) %all-gather.5.cloned.1.call-update) | async-done | bytes 3211280 | tf_op jit(solution)/shard_map/all_gather | solution.py:91
  551.9 6.7 convolution_bitcast_fusion.3
  558.6 30.6 %all-reduce.6.cloned.1.call-done = f32[256,128]{0,1:T(8,128)} async-done(((f32[256,128]{0,1:T(8,128)}), f32[256,128]{0,1:T(8,128)}) %all-reduce.6.cloned.1.call-update) | async-done | bytes 131088 | tf_op jit(solution)/shard_map/psum | solution.py:88
  589.2 0.9 broadcast_multiply_fusion
  590.1 3.4 collective-permute-start.4
  593.5 1.2 fusion.8
  594.7 0.7 collective-permute-done.4
  595.4 0.3 fusion
  595.7 1.3 collective-permute-start.5
  597.0 0.3 fusion.38
  597.3 4.9 collective-permute-done.5
  602.2 0.3 convolution_add_fusion
  602.6 6.5 convolution_bitcast_fusion
  609.2 8.0 %copy.78 = f32[12544,128]{1,0:T(8,128)} copy(f32[12544,128]{0,1:T(8,128)} %convolution_bitcast_fusion) | data formatting | bytes 12845056
  617.2 120.6 %reduce-scatter.14.cloned.1.call-done = f32[1568,128]{1,0:T(8,128)} async-done(((f32[12544,128]{1,0:T(8,128)}), f32[1568,128]{1,0:T(8,128)}) %reduce-scatter.14.cloned.1.call-update) | async-done | bytes 802832
  737.8 1.4 copy.79
  739.2 0.5 multiply_reduce_fusion
  739.7 39.5 %psum.47 = f32[128]{0:T(128)S(1)} all-reduce(f32[128]{0:T(128)S(1)} %multiply_reduce_fusion), channel_id=1, replica_groups=mesh['tm'=8,'coef'=4] {'tm','coef'}, use_global_device_ids=true, to_apply=%region_12.0 | all-reduce | flops 128 | bytes 1024 | tf_op jit(solution)/shard_map/psum | solution.py:74
  779.2 1.5 multiply_subtract_fusion
  780.7 2.3 copy.52
  783.0 1.2 copy.51
  (33 shorter events, 1.0 us)
Async XLA Ops:
  7.2 152.8 %reduce-scatter.10.cloned.1.call-start = ((), (), s32[]{:S(2)}) async-start(), calls=%async_computation.7 | async-start | bytes 7225344
  9.6 7.6 collective-permute-start
  17.5 6.2 collective-permute-start.1
  38.6 184.0 %all-gather.3.cloned.1.call-start = ((), (), s32[]{:S(2)}) async-start(), calls=%async_computation.3 | async-start | bytes 3612672 | tf_op jit(solution)/shard_map/all_gather | solution.py:91
  162.4 97.5 %all-reduce.4.cloned.1.call-start = ((), (), s32[]{:S(2)}) async-start(), calls=%async_computation.4 | async-start | bytes 262144 | tf_op jit(solution)/shard_map/psum | solution.py:88
  229.3 179.1 %reduce-scatter.12.cloned.1.call-start = ((), (), s32[]{:S(2)}) async-start(), calls=%async_computation.8 | async-start | bytes 7225344
  260.8 5.3 collective-permute-start.2
  266.4 6.5 collective-permute-start.3
  287.8 264.0 %all-gather.5.cloned.1.call-start = ((), (), s32[]{:S(2)}) async-start(), calls=%async_computation.5 | async-start | bytes 3612672 | tf_op jit(solution)/shard_map/all_gather | solution.py:91
  490.9 98.3 %all-reduce.6.cloned.1.call-start = ((), (), s32[]{:S(2)}) async-start(), calls=%async_computation.6 | async-start | bytes 262144 | tf_op jit(solution)/shard_map/psum | solution.py:88
  558.6 179.2 %reduce-scatter.14.cloned.1.call-start = ((), (), s32[]{:S(2)}) async-start(), calls=%async_computation.9 | async-start | bytes 7225344
  590.1 5.3 collective-permute-start.4
  595.7 6.5 collective-permute-start.5
Sparse Core Ops, SparseCore 0:
  38.7 121.1 reduce-scatter.9
  162.7 59.8 all-gather.2
  229.4 30.4 all-reduce.3
  288.0 120.4 reduce-scatter.11
  491.1 60.7 all-gather.4
  558.7 30.4 all-reduce.5
  617.3 120.4 reduce-scatter.13
where the time goes:
time: 792 us; the launch traced here: 791 us
  waiting for transfers between devices  559 us (71%)
  blocking collectives  119 us (15%)
  matrix products  38.3 us (5%)
  local copies, waits for them, and re-layouts  38.1 us (5%)
  starting transfers between devices  16 us (2%)
  between operations  15.1 us (2%)
    unnamed x10, waiting for transfers between devices  361 us
    all_gather x2, waiting for transfers between devices, shards(): lax.all_gather(direction.astype(jnp.bfloat16), 'tm', axis=0, tiled=True)  121 us
    psum x3, blocking collectives, global_sum(): return lax.psum(terms, ('tm', 'coef'))  119 us
    psum x2, waiting for transfers between devices, shards(): lax.psum(jnp.dot(design, lax.all_gather(direction.astype(jnp.bfloat16), '...  61.1 us
    unnamed x12, local copies, waits for them, and re-layouts  32.9 us
    dot_general x3, matrix products, transposed_term(): lax.dot_general(design, filtered, (((0,), (0,)), ((), ())), preferred_ele...  19.6 us
  transfers between devices with their start and end apart: 13, of which 12 were waited for; matrix products, arithmetic and copies ran while one was open for 1% of the time, Pallas kernels for 0%

commit v1 on v0

--- a/solution.py
+++ b/solution.py
@@ -85,13 +85,16 @@
     direction = scaled
     norm_now = global_sum(jnp.sum(residual * scaled, 0))
     for iteration in range(ITERS):
-        slab_values = lax.psum(
-            jnp.dot(
-                design,
-                lax.all_gather(direction.astype(jnp.bfloat16), "tm", axis=0, tiled=True),
-                preferred_element_type=jnp.float32,
+        slab_values = jnp.sum(
+            lax.all_gather(
+                jnp.dot(
+                    design,
+                    lax.all_gather(direction.astype(jnp.bfloat16), "tm", axis=0, tiled=True),
+                    preferred_element_type=jnp.float32,
+                ),
+                "coef",
             ),
-            "coef",
+            axis=0,
         )
         image = collect_rows(weighted(slab_values)) + kaula_col * direction
         curvature = global_sum(jnp.sum(direction * image, 0))

time: 792 us -> 742 us (0.937)
  waiting for transfers between devices: 559 us -> 500 us
  blocking collectives: 119 us -> 133 us
    psum x2 -> x0, waiting for transfers between devices: 61.1 us -> none  [shards(): lax.psum(jnp.dot(design, lax.all_gather(direction.astype(jnp.bfloat16), '...]
    all_gather x0 -> x2, blocking collectives: none -> 14.3 us  [shards(): lax.all_gather(jnp.dot(design, lax.all_gather(direction.astype(jnp.bfloat...]
    unnamed x10 -> x8, waiting for transfers between devices: 361 us -> 362 us
    unnamed x12 -> x14, local copies, waits for them, and re-layouts: 32.9 us -> 32.9 us
  transfers between devices with their start and end apart: 13 -> 11, of which waited for: 12 -> 10; matrix products, arithmetic and copies ran while one was open for 1% -> 1% of each run, Pallas kernels for 0% -> 0%
where the time goes in v1:
time: 742 us; the launch traced here: 741 us
  waiting for transfers between devices  500 us (67%)
  blocking collectives  133 us (18%)
  local copies, waits for them, and re-layouts  38.6 us (5%)
  matrix products  35.2 us (5%)
  between operations  14.8 us (2%)
  starting transfers between devices  14.1 us (2%)
    unnamed x8, waiting for transfers between devices  362 us
    all_gather x2, waiting for transfers between devices, shards(): lax.all_gather(direction.astype(jnp.bfloat16), 'tm', axis=0, tiled=True)  121 us
    psum x3, blocking collectives, global_sum(): return lax.psum(terms, ('tm', 'coef'))  119 us
    unnamed x14, local copies, waits for them, and re-layouts  32.9 us
    dot_general x3, matrix products, transposed_term(): lax.dot_general(design, filtered, (((0,), (0,)), ((), ())), preferred_ele...  19.6 us
    ppermute x6, waiting for transfers between devices, shifted(): lax.ppermute(value, axis, [(source, source + steps) for source in range(f...  17.7 us
  transfers between devices with their start and end apart: 11, of which 10 were waited for; matrix products, arithmetic and copies ran while one was open for 1% of the time, Pallas kernels for 0%

profile of v1, /device:TPU:0, one launch (start us, length us, event | category | flops | bytes accessed | tf_op | source)
XLA Modules:
  0.0 741.0 jit_solution(13712562836502647577)
XLA Ops:
  7.9 1.0 copy.30
  8.9 0.7 and_convert_fusion
  9.6 4.9 collective-permute-start
  14.5 0.7 slice.67
  15.3 0.7 pad_maximum_fusion.1
  16.1 0.3 reshape.52
  16.5 0.3 fusion.12
  16.8 0.3 reshape.53
  17.2 0.3 fusion.2
  17.5 1.3 collective-permute-start.1
  18.8 0.3 fusion.40
  19.1 4.5 collective-permute-done.1
  23.7 0.3 convolution_add_fusion.4
  24.1 6.5 convolution_bitcast_fusion.2
  30.6 8.0 %copy.74 = f32[12544,128]{1,0:T(8,128)} copy(f32[12544,128]{0,1:T(8,128)} %convolution_bitcast_fusion.2) | data formatting | bytes 12845056
  38.7 0.8 dynamic_slice.6
  39.5 120.8 %reduce-scatter.10.cloned.1.call-done = f32[1568,128]{1,0:T(8,128)} async-done(((f32[12544,128]{1,0:T(8,128)}), f32[1568,128]{1,0:T(8,128)}) %reduce-scatter.10.cloned.1.call-update) | async-done | bytes 802832
  160.3 1.4 copy.75
  161.8 0.9 copy.37
  162.8 60.1 %all-gather.5.cloned.1.call-done = bf16[12544,128]{1,0:T(8,128)(2,1)} async-done(((bf16[1568,128]{1,0:T(8,128)(2,1)}), bf16[12544,128]{1,0:T(8,128)(2,1)}) %all-gather.5.cloned.1.call-update) | async-done | bytes 3211280 | tf_op jit(solution)/shard_map/all_gather | solution.py:92
  223.0 6.0 convolution_bitcast_fusion.4
  229.0 7.1 all-gather
  236.4 0.3 reduce_sum.59
  236.8 2.5 collective-permute-start.2
  239.2 0.3 fusion.10
  239.5 1.6 collective-permute-done.2
  241.1 0.3 fusion.1
  241.4 1.3 collective-permute-start.3
  242.7 0.3 fusion.39
  243.0 5.0 collective-permute-done.3
  248.0 0.3 convolution_add_fusion.2
  248.4 6.5 convolution_bitcast_fusion.1
  255.0 8.0 %copy.76 = f32[12544,128]{1,0:T(8,128)} copy(f32[12544,128]{0,1:T(8,128)} %convolution_bitcast_fusion.1) | data formatting | bytes 12845056
  263.0 0.8 dynamic_slice.7
  263.8 120.0 %reduce-scatter.12.cloned.1.call-done = f32[1568,128]{1,0:T(8,128)} async-done(((f32[12544,128]{1,0:T(8,128)}), f32[1568,128]{1,0:T(8,128)}) %reduce-scatter.12.cloned.1.call-update) | async-done | bytes 802832
  383.8 1.4 copy.77
  385.3 0.3 fusion.5
  385.6 39.5 %all-reduce = (f32[128]{0:T(128)S(1)}, f32[128]{0:T(128)S(1)}) all-reduce(f32[128]{0:T(128)S(1)} %get-tuple-element.7, f32[128]{0:T(128)S(1)} %get-tuple-element.6), channel_id=1, replica_groups=mesh['tm'=8,'coef'=4] {'tm','coef'}, use_global_device_ids=true, to_apply=%region_2.0 | all-reduce | flops 256 | bytes 2048 | tf_op jit(solution)/shard_map/psum | solution.py:74
  425.1 0.3 fusion.7
  425.4 39.6 %psum.30 = f32[128]{0:T(128)S(1)} all-reduce(f32[128]{0:T(128)S(1)} %fusion.7), channel_id=1, replica_groups=mesh['tm'=8,'coef'=4] {'tm','coef'}, use_global_device_ids=true, to_apply=%region_8.0 | all-reduce | flops 128 | bytes 1024 | tf_op jit(solution)/shard_map/psum | solution.py:74
  465.0 0.3 fusion.47
  465.4 0.9 copy.44
  466.6 60.7 %all-gather.7.cloned.1.call-done = bf16[12544,128]{1,0:T(8,128)(2,1)} async-done(((bf16[1568,128]{1,0:T(8,128)(2,1)}), bf16[12544,128]{1,0:T(8,128)(2,1)}) %all-gather.7.cloned.1.call-update) | async-done | bytes 3211280 | tf_op jit(solution)/shard_map/all_gather | solution.py:92
  527.3 6.0 convolution_bitcast_fusion.3
  533.3 7.1 all-gather.1
  540.4 0.2 reshape.58
  540.7 0.3 reduce_sum.63
  541.0 2.5 collective-permute-start.4
  543.5 0.3 fusion.8
  543.8 1.6 collective-permute-done.4
  545.4 0.3 fusion
  545.7 1.3 collective-permute-start.5
  547.0 0.3 fusion.38
  547.3 5.0 collective-permute-done.5
  552.3 0.3 convolution_add_fusion
  552.7 6.5 convolution_bitcast_fusion
  559.2 8.0 %copy.78 = f32[12544,128]{1,0:T(8,128)} copy(f32[12544,128]{0,1:T(8,128)} %convolution_bitcast_fusion) | data formatting | bytes 12845056
  567.2 120.9 %reduce-scatter.14.cloned.1.call-done = f32[1568,128]{1,0:T(8,128)} async-done(((f32[12544,128]{1,0:T(8,128)}), f32[1568,128]{1,0:T(8,128)}) %reduce-scatter.14.cloned.1.call-update) | async-done | bytes 802832
  688.1 1.4 copy.79
  689.5 0.5 multiply_reduce_fusion
  690.0 39.5 %psum.31 = f32[128]{0:T(128)S(1)} all-reduce(f32[128]{0:T(128)S(1)} %multiply_reduce_fusion), channel_id=1, replica_groups=mesh['tm'=8,'coef'=4] {'tm','coef'}, use_global_device_ids=true, to_apply=%region_12.0 | all-reduce | flops 128 | bytes 1024 | tf_op jit(solution)/shard_map/psum | solution.py:74
  729.5 1.5 multiply_subtract_fusion
  731.0 2.3 copy.52
  733.4 1.2 copy.51
  (36 shorter events, 1.4 us)
Async XLA Ops:
  7.2 153.1 %reduce-scatter.10.cloned.1.call-start = ((), (), s32[]{:S(2)}) async-start(), calls=%async_computation.5 | async-start | bytes 7225344
  9.6 7.6 %collective-permute-start = (f32[128,128]{0,1:T(8,128)S(1)}, f32[128,128]{0,1:T(8,128)S(1)}, u32[]{:S(2)}, u32[]{:S(2)}) collective-permute-start(f32[128,128]{0,1:T(8,128)S(1)} %get-tuple-element.22), channel_id=1, source_target_pairs={{0,4},{4,8},{8,12},{12,16},{16,20},{20,24},{24,28},{1,5},{5,9},{9,... | collective-permute-start | bytes 196616 | tf_op jit(solution)/shard_map/ppermute | solution.py:12
  17.5 6.2 collective-permute-start.1
  38.6 124.2 %copy-start = (s32[256]{0:T(256)S(1)}, s32[256]{0:T(256)}, u32[]{:S(2)}) copy-start(s32[256]{0:T(256)} %param.10) | copy-start | bytes 3076
  38.6 184.4 %all-gather.5.cloned.1.call-start = ((), (), s32[]{:S(2)}) async-start(), calls=%async_computation.3 | async-start | bytes 3612672 | tf_op jit(solution)/shard_map/all_gather | solution.py:92
  162.8 221.1 %reduce-scatter.12.cloned.1.call-start = ((), (), s32[]{:S(2)}) async-start(), calls=%async_computation.6 | async-start | bytes 7225344
  236.8 4.3 collective-permute-start.2
  241.4 6.6 collective-permute-start.3
  263.0 264.3 %all-gather.7.cloned.1.call-start = ((), (), s32[]{:S(2)}) async-start(), calls=%async_computation.4 | async-start | bytes 3612672 | tf_op jit(solution)/shard_map/all_gather | solution.py:92
  466.3 221.8 %reduce-scatter.14.cloned.1.call-start = ((), (), s32[]{:S(2)}) async-start(), calls=%async_computation.7 | async-start | bytes 7225344
  541.0 4.3 collective-permute-start.4
  545.7 6.6 collective-permute-start.5
Sparse Core Ops, SparseCore 0:
  38.7 121.5 reduce-scatter.9
  163.1 59.8 all-gather.4
  263.1 120.7 reduce-scatter.11
  466.5 60.7 all-gather.6
  567.4 120.7 reduce-scatter.13
